TPU v7x, 32 devices: a 4x2x2 block of a 4x4x8 slice. The times are simulated.
32 devices in a mesh: stage: 4 (over y, z), data: 8 (over x, core).
Axes of the slice: x: 4, y: 2, z: 2, core: 2. Of those that a mesh axis runs over, the one named last changes fastest.
The devices are a block of a 4x4x8 slice.
Arguments:
- w_master: float32 [192, 512, 512], P('stage', 'data'), parts along dimension 0
- momentum: float32 [192, 512, 512], P('stage', 'data'), parts along dimension 0
- grads: bfloat16 [32, 48, 512, 512], P(('stage', 'data')), parts along dimension 0
Outputs:
- output 1: float32 [192, 512, 512], P('stage', 'data'), parts along dimension 0
- output 2: float32 [192, 512, 512], P('stage', 'data'), parts along dimension 0
There are 4 independent parts. A program takes and returns all parts, laid end to end along the dimension named above; each array names one.
All inputs are finite; a program needn't handle non-finite values.
Results may differ from a plain program's by a relative error of at most 0.0147327.
Values are sent between devices in bfloat16 or wider.
A program may use at most 768 MiB of HBM per device.

v0:
```python
import math
import jax
import jax.numpy as jnp
from jax import lax
from jax.sharding import PartitionSpec as P, NamedSharding

MOMENTUM_COEF = 0.95
LEARN_RATE = 0.05
WEIGHT_DECAY = 0.2
NORM_EPS = 1e-7
COEF_A = 3.4445
COEF_B = -4.7750
COEF_C = 2.0315
NS_ITERS = 5


def newton_schulz(x_cur):
    n_rows, n_cols = x_cur.shape[1], x_cur.shape[2]
    for _ in range(NS_ITERS):
        if n_rows > n_cols:
            gram_f = jnp.einsum('bri,brj->bij', x_cur, x_cur, preferred_element_type=jnp.float32)
        else:
            gram_f = jnp.einsum('bik,bjk->bij', x_cur, x_cur, preferred_element_type=jnp.float32)
        gram_mat = gram_f.astype(jnp.bfloat16)
        gram_sq = jnp.einsum('bij,bjk->bik', gram_mat, gram_mat, preferred_element_type=jnp.float32)
        poly_mat = (COEF_B * gram_mat.astype(jnp.float32) + COEF_C * gram_sq).astype(jnp.bfloat16)
        if n_rows > n_cols:
            poly_x = jnp.einsum('brj,bij->bri', x_cur, poly_mat, preferred_element_type=jnp.float32)
        else:
            poly_x = jnp.einsum('bij,bjk->bik', poly_mat, x_cur, preferred_element_type=jnp.float32)
        x_cur = (COEF_A * x_cur.astype(jnp.float32) + poly_x).astype(jnp.bfloat16)
    return x_cur


def solution(mesh):
    group_size = mesh.shape['data']
    row_spec = P('stage', 'data', None)
    grad_spec = P(('stage', 'data'), None, None, None)

    def local_step(w_rows, mom_rows, grad_full):
        n_mats, rows_dev, n_cols = w_rows.shape
        n_rows = rows_dev * group_size
        per_dev = n_mats // group_size
        my_index = lax.axis_index('data')
        grad_rows = lax.psum_scatter(grad_full[0].astype(jnp.float32), 'data', scatter_dimension=1, tiled=True)
        mom_new = MOMENTUM_COEF * mom_rows + grad_rows
        frob_norm = jnp.sqrt(lax.psum(jnp.sum(mom_new * mom_new, axis=(1, 2)), 'data'))
        owned_mom = lax.all_to_all(mom_new.astype(jnp.bfloat16), 'data', 0, 1, tiled=True)
        owned_norm = lax.dynamic_slice_in_dim(frob_norm, my_index * per_dev, per_dev)
        x_start = (owned_mom.astype(jnp.float32) / (owned_norm[:, None, None] + NORM_EPS)).astype(jnp.bfloat16)
        x_ortho = newton_schulz(x_start)
        x_rows = lax.all_to_all(x_ortho, 'data', 1, 0, tiled=True)
        rms_scale = 0.2 * math.sqrt(max(n_rows, n_cols))
        w_new = w_rows - LEARN_RATE * (x_rows.astype(jnp.float32) * rms_scale + WEIGHT_DECAY * w_rows)
        return w_new, mom_new

    return jax.shard_map(local_step, mesh=mesh, in_specs=(row_spec, row_spec, grad_spec), out_specs=(row_spec, row_spec), check_vma=False)
```

profile of v0, /device:TPU:81, one launch (start us, length us, event | category | flops | bytes accessed | tf_op | source)
XLA Modules:
  0.0 490.0 jit_solution(16327761097525111516)
XLA Ops:
  7.2 0.1 reduce-scatter.2.cloned.1.call-start
  7.2 27.0 %bitcast_convert_fusion = f32[48,512,512]{2,1,0:T(8,128)} fusion(bf16[1,48,512,512]{3,2,1,0:T(8,128)(2,1)} %param.5), kind=kLoop, calls=%fused_computation | loop fusion | flops 12582912 | bytes 75497472 | tf_op jit(solution)/shard_map/convert_element_type | solution.py:45
  34.3 0.1 reduce-scatter.2.cloned.1.call-update
  34.3 250.2 %reduce-scatter.2.cloned.1.call-done = f32[48,64,512]{2,1,0:T(8,128)} async-done(((f32[48,512,512]{2,1,0:T(8,128)}), f32[48,64,512]{2,1,0:T(8,128)}) %reduce-scatter.2.cloned.1.call-update) | async-done | bytes 6291472 | tf_op jit(solution)/shard_map/reduce_scatter | solution.py:45
  284.5 5.8 %multiply_reduce_fusion = (f32[48]{0:T(128)S(1)}, f32[48,64,512]{2,1,0:T(8,128)S(1)}) fusion(f32[48,64,512]{2,1,0:T(8,128)} %reduce-scatter.2.cloned.1.call-done, f32[48,64,512]{2,1,0:T(8,128)} %param.4), kind=kLoop, calls=%fused_computation.17 | loop fusion | flops 6291408 | bytes 18874560 | tf_op jit(solution)/shard_map/reduce_sum | solution.py:47
  290.3 2.7 copy-done
  293.0 2.1 convert_element_type.107
  295.2 4.6 all-to-all-start
  299.8 41.9 %psum.7 = f32[48]{0:T(128)S(1)} all-reduce(f32[48]{0:T(128)S(1)} %get-tuple-element.2), channel_id=1, replica_groups=mesh['stage'=4,'data'=8] {'data'}, use_global_device_ids=true, to_apply=%region_2.0 | all-reduce | flops 48 | bytes 384 | tf_op jit(solution)/shard_map/psum | solution.py:47
  341.8 0.1 dynamic-slice_add_fusion
  341.8 0.0 all-to-all-done
  341.8 0.8 copy.7
  342.7 1.0 fusion
  343.7 3.5 convolution_convert_fusion.4
  347.2 8.9 %add_convert_fusion.8 = bf16[6,512,512]{2,1,0:T(8,128)(2,1)} fusion(bf16[6,512,512]{2,1,0:T(8,128)(2,1)S(1)} %fusion, bf16[6,512,512]{2,1,0:T(8,128)(2,1)} %convolution_convert_fusion.4), kind=kOutput, calls=%fused_computation.15 | convolution fusion | flops 3235381248 | bytes 9437184 | tf_op jit(solution)/shard_map/bij,bjk->bik/dot_general | solution.py:30
  356.1 6.5 %convolution_convert_fusion.3 = bf16[6,512,512]{2,1,0:T(8,128)(2,1)} fusion(bf16[6,512,512]{2,1,0:T(8,128)(2,1)} %add_convert_fusion.8), kind=kOutput, calls=%fused_computation.37 | convolution fusion | flops 1612185600 | bytes 6291456 | tf_op jit(solution)/shard_map/bik,bjk->bij/dot_general | solution.py:23
  362.6 0.0 copy-done.1
  362.6 8.9 %add_convert_fusion.6 = bf16[6,512,512]{2,1,0:T(8,128)(2,1)} fusion(bf16[6,512,512]{2,1,0:T(8,128)(2,1)S(1)} %copy-done.1, bf16[6,512,512]{2,1,0:T(8,128)(2,1)} %convolution_convert_fusion.3), kind=kOutput, calls=%fused_computation.13 | convolution fusion | flops 3235381248 | bytes 9437184 | tf_op jit(solution)/shard_map/bij,bjk->bik/dot_general | solution.py:30
  371.5 6.5 %convolution_convert_fusion.2 = bf16[6,512,512]{2,1,0:T(8,128)(2,1)} fusion(bf16[6,512,512]{2,1,0:T(8,128)(2,1)} %add_convert_fusion.6), kind=kOutput, calls=%fused_computation.36 | convolution fusion | flops 1612185600 | bytes 6291456 | tf_op jit(solution)/shard_map/bik,bjk->bij/dot_general | solution.py:23
  377.9 0.0 copy-done.2
  377.9 9.1 %add_convert_fusion.4 = bf16[6,512,512]{2,1,0:T(8,128)(2,1)} fusion(bf16[6,512,512]{2,1,0:T(8,128)(2,1)S(1)} %copy-done.2, bf16[6,512,512]{2,1,0:T(8,128)(2,1)} %convolution_convert_fusion.2), kind=kOutput, calls=%fused_computation.11 | convolution fusion | flops 3235381248 | bytes 9437184 | tf_op jit(solution)/shard_map/bij,bjk->bik/dot_general | solution.py:30
  387.1 6.5 %convolution_convert_fusion.1 = bf16[6,512,512]{2,1,0:T(8,128)(2,1)} fusion(bf16[6,512,512]{2,1,0:T(8,128)(2,1)} %add_convert_fusion.4), kind=kOutput, calls=%fused_computation.35 | convolution fusion | flops 1612185600 | bytes 6291456 | tf_op jit(solution)/shard_map/bik,bjk->bij/dot_general | solution.py:23
  393.6 0.0 copy-done.3
  393.6 8.9 %add_convert_fusion.2 = bf16[6,512,512]{2,1,0:T(8,128)(2,1)} fusion(bf16[6,512,512]{2,1,0:T(8,128)(2,1)S(1)} %copy-done.3, bf16[6,512,512]{2,1,0:T(8,128)(2,1)} %convolution_convert_fusion.1), kind=kOutput, calls=%fused_computation.9 | convolution fusion | flops 3235381248 | bytes 9437184 | tf_op jit(solution)/shard_map/bij,bjk->bik/dot_general | solution.py:30
  402.5 6.3 %convolution_convert_fusion = bf16[6,512,512]{2,1,0:T(8,128)(2,1)} fusion(bf16[6,512,512]{2,1,0:T(8,128)(2,1)} %add_convert_fusion.2), kind=kOutput, calls=%fused_computation.34 | convolution fusion | flops 1612185600 | bytes 6291456 | tf_op jit(solution)/shard_map/bik,bjk->bij/dot_general | solution.py:23
  408.8 9.1 %add_convert_fusion = bf16[6,512,512]{2,1,0:T(8,128)(2,1)S(1)} fusion(bf16[6,512,512]{2,1,0:T(8,128)(2,1)} %add_convert_fusion.2, bf16[6,512,512]{2,1,0:T(8,128)(2,1)} %convolution_convert_fusion), kind=kOutput, calls=%fused_computation.7 | convolution fusion | flops 3235381248 | bytes 9437184 | tf_op jit(solution)/shard_map/bij,bjk->bik/dot_general | solution.py:30
  417.9 2.1 copy.8
  420.0 53.4 %all_to_all.8 = bf16[6,512,512]{2,0,1:T(8,128)(2,1)S(1)} all-to-all(bf16[6,512,512]{2,0,1:T(8,128)(2,1)S(1)} %copy.8), channel_id=1, replica_groups=mesh['stage'=4,'data'=8] {'data'}, dimensions={1} | all-to-all | bytes 6291456 | tf_op jit(solution)/shard_map/all_to_all | solution.py:52
  473.4 1.3 convert_multiply_fusion
  474.7 0.0 slice-start.1
  474.7 3.6 copy.9
  478.3 4.9 fusion.2
  (9 shorter events, 0.0 us)
Async XLA Ops:
  7.2 277.3 %reduce-scatter.2.cloned.1.call-start = ((), (), s32[]{:S(2)}) async-start(), calls=%async_computation.3 | async-start | bytes 56623104 | tf_op jit(solution)/shard_map/reduce_scatter | solution.py:45
  290.3 2.7 copy-start
  295.2 46.6 %all-to-all-start = ((bf16[48,64,512]{2,1,0:T(8,128)(2,1)}), bf16[48,64,512]{2,1,0:T(8,128)(2,1)S(1)}, u32[]{:S(2)}, u32[]{:S(2)}) async-start(bf16[48,64,512]{2,1,0:T(8,128)(2,1)} %convert_element_type.107), calls=%async_computation.1 | async-start | bytes 6291456 | tf_op jit(solution)/shard_map/all_to_all | solution.py:48
  356.1 6.5 %copy-start.1 = (bf16[6,512,512]{2,1,0:T(8,128)(2,1)S(1)}, bf16[6,512,512]{2,1,0:T(8,128)(2,1)}, u32[]{:S(2)}) copy-start(bf16[6,512,512]{2,1,0:T(8,128)(2,1)} %add_convert_fusion.8) | copy-start | bytes 9437188
  371.5 6.5 %copy-start.2 = (bf16[6,512,512]{2,1,0:T(8,128)(2,1)S(1)}, bf16[6,512,512]{2,1,0:T(8,128)(2,1)}, u32[]{:S(2)}) copy-start(bf16[6,512,512]{2,1,0:T(8,128)(2,1)} %add_convert_fusion.6) | copy-start | bytes 9437188
  387.1 6.5 %copy-start.3 = (bf16[6,512,512]{2,1,0:T(8,128)(2,1)S(1)}, bf16[6,512,512]{2,1,0:T(8,128)(2,1)}, u32[]{:S(2)}) copy-start(bf16[6,512,512]{2,1,0:T(8,128)(2,1)} %add_convert_fusion.4) | copy-start | bytes 9437188
  473.4 4.8 slice-start
  474.7 3.6 slice-start.1
Sparse Core Ops, SparseCore 0:
  34.5 250.0 reduce-scatter.1
where the time goes:
time: 490 us
  waiting for transfers between devices  250 us (51%)
  blocking collectives  95.3 us (19%)
  matrix products  74.2 us (15%)
  other arithmetic  42.2 us (9%)
  between operations  14.2 us (3%)
  local copies, waits for them, and re-layouts  9.23 us (2%)
    reduce_scatter x1, waiting for transfers between devices, local_step(): lax.psum_scatter(grad_full[0].astype(jnp.float32), 'data', scatter_dimens...  250 us
    all_to_all x1, blocking collectives, local_step(): x_rows = lax.all_to_all(x_ortho, 'data', 1, 0, tiled=True)  53.4 us
    dot_general x5, matrix products, newton_schulz(): jnp.einsum('bij,bjk->bik', poly_mat, x_cur, preferred_element_type=jnp.fl...  44.9 us
    psum x1, blocking collectives, local_step(): lax.psum(jnp.sum(mom_new * mom_new, axis=(1, 2)), 'data')  41.9 us
    dot_general x5, matrix products, newton_schulz(): jnp.einsum('bik,bjk->bij', x_cur, x_cur, preferred_element_type=jnp.float32)  29.3 us
    convert_element_type x1, other arithmetic, local_step(): grad_full[0].astype(jnp.float32)  27 us
  transfers between devices with their start and end apart: 2, of which 1 were waited for; matrix products, arithmetic and copies ran while one was open for 0% of the time, Pallas kernels for 0%

commit v1 on v0

v1 whole, which is shorter than its diff:
```python
import functools
import math
import jax
import jax.numpy as jnp
from jax import lax
from jax.experimental import pallas as pl
from jax.experimental.pallas import tpu as pltpu
from jax.sharding import PartitionSpec as P

MOMENTUM_COEF = 0.95
LEARN_RATE = 0.05
WEIGHT_DECAY = 0.2
NORM_EPS = 1e-7
COEF_A = 3.4445
COEF_B = -4.7750
COEF_C = 2.0315
NS_ITERS = 5
F32 = jnp.float32
BF16 = jnp.bfloat16


def muon_kernel(G, R, g_ref, w_ref, m_ref, wn_ref, mn_ref,
                rl, orl, fo, fi, dr, po, ow, mi, mo, mb, mr, nso, nr, xo, orr, wi, wo, a_s, b_s,
                s_rl, s_fi, s_dr, s_po, s_mr, s_nr, s_or,
                t_raw, t_fo, t_m, t_n, t_o,
                l_rl, l_ow, l_m, l_w, l_mo, l_wo):
    NM = G
    RB = mi.shape[2]
    H = RB // 2
    C = mi.shape[3]
    scale = 0.2 * math.sqrt(max(G * RB, C))
    chips = G // 2
    d = lax.axis_index('data')
    p = d // 2
    c = lax.rem(d, 2)
    right = lax.rem(p + 1, chips)
    left = lax.rem(p + chips - 1, chips)
    opp = lax.rem(p + 2, chips)
    partner = 2 * p + (1 - c)

    def remote(src, dst, ssem, rsem, dev):
        pltpu.make_async_remote_copy(src_ref=src, dst_ref=dst, send_sem=ssem, recv_sem=rsem,
                                     device_id={'data': dev}, device_id_type=pl.DeviceIdType.MESH).start()

    def drain(ref, sem):
        pltpu.make_async_copy(ref, ref, sem).wait()

    def mats(r):
        return pl.ds(r * NM, NM)

    def grows(r, dev, half):
        return g_ref.at[mats(r), pl.ds(pl.multiple_of(dev * RB + half * H, H), H), :]

    def load_relay(r):
        s = r % 2
        pltpu.make_async_copy(grows(r, 2 * right + c, 0), orl.at[s, 0], l_rl.at[r]).start()
        pltpu.make_async_copy(grows(r, 2 * left + c, 1), orl.at[s, 1], l_rl.at[r]).start()

    def load_final(r):
        s = r % 2
        pltpu.make_async_copy(g_ref.at[mats(r), pl.ds(pl.multiple_of(d * RB, RB), RB), :], ow.at[s], l_ow.at[r]).start()
        pltpu.make_async_copy(m_ref.at[mats(r)], mi.at[s], l_m.at[r]).start()

    def load_w(r):
        pltpu.make_async_copy(w_ref.at[mats(r)], wi.at[r % 2], l_w.at[r]).start()

    def raw(r):
        for cc in range(2):
            remote(grows(r, 2 * opp + cc, 0), rl.at[r, 0, c], t_raw.at[r], s_rl.at[r, 0], 2 * right + cc)
            remote(grows(r, 2 * opp + cc, 1), rl.at[r, 1, c], t_raw.at[r], s_rl.at[r, 1], 2 * left + cc)
        remote(grows(r, 2 * right + (1 - c), 0), rl.at[r, 0, 2], t_raw.at[r], s_rl.at[r, 0], partner)
        remote(grows(r, 2 * left + (1 - c), 1), rl.at[r, 1, 2], t_raw.at[r], s_rl.at[r, 1], partner)
        for cc in range(2):
            remote(grows(r, 2 * right + cc, 1), dr.at[r, 0, c], t_raw.at[r], s_dr.at[r], 2 * right + cc)
            remote(grows(r, 2 * left + cc, 0), dr.at[r, 1, c], t_raw.at[r], s_dr.at[r], 2 * left + cc)
        remote(g_ref.at[mats(r), pl.ds(pl.multiple_of(partner * RB, RB), RB), :], po.at[r], t_raw.at[r], s_po.at[r], partner)

    def relay(r):
        s = r % 2
        drain(orl.at[s], l_rl.at[r])
        for q in range(2):
            drain(rl.at[r, q], s_rl.at[r, q])
            if r >= 2:
                drain(fo.at[s, q], t_fo.at[r - 2, q])

            def body(k, _):
                fo[s, q, k] = ((rl[r, q, 0, k].astype(F32) + rl[r, q, 1, k].astype(F32))
                               + (rl[r, q, 2, k].astype(F32) + orl[s, q, k].astype(F32)))
                return 0
            lax.fori_loop(0, NM, body, 0)
            remote(fo.at[s, q], fi.at[r, q], t_fo.at[r, q], s_fi.at[r, q], 2 * (right if q == 0 else left) + c)
        if r + 2 < R:
            load_relay(r + 2)

    def final(r):
        s = r % 2
        drain(ow.at[s], l_ow.at[r])
        drain(mi.at[s], l_m.at[r])
        drain(po.at[r], s_po.at[r])
        drain(dr.at[r], s_dr.at[r])
        for q in range(2):
            drain(fi.at[r, q], s_fi.at[r, q])
        if r >= 2:
            drain(mo.at[s], l_mo.at[r - 2])

        def body(k, _):
            part = jnp.zeros((8, 128), F32)
            for q in range(2):
                rows = pl.ds(q * H, H)
                grad = ((dr[r, 1 - q, 0, k].astype(F32) + dr[r, 1 - q, 1, k].astype(F32))
                        + (po[r, k, rows, :].astype(F32) + ow[s, k, rows, :].astype(F32))) + fi[r, q, k]
                new = MOMENTUM_COEF * mi[s, k, rows, :] + grad
                mo[s, k, rows, :] = new
                mb[r, k, rows, :] = new.astype(BF16)
                sq = jnp.sum((new * new).reshape(H // 8, 8, C), axis=0)
                for j in range(C // 128):
                    part = part + sq[:, j * 128:(j + 1) * 128]
            nso[r, k] = part
            return 0
        lax.fori_loop(0, NM, body, 0)
        mine = pl.ds(pl.multiple_of(d * RB, RB), RB)
        for j in range(1, G):
            dev = lax.rem(d + j, G)
            remote(nso.at[r, dev], nr.at[r, d], t_n.at[r], s_nr.at[r], dev)
            remote(mb.at[r, dev], mr.at[r, mine, :], t_m.at[r], s_mr.at[r], dev)
        mr[r, mine, :] = mb[r, d]
        nr[r, d] = nso[r, d]
        pltpu.make_async_copy(mo.at[s], mn_ref.at[mats(r)], l_mo.at[r]).start()
        if r + 2 < R:
            load_final(r + 2)

    def ns(r):
        drain(nr.at[r, pl.ds(0, G - 1)], s_nr.at[r])
        drain(mr.at[r, pl.ds(0, (G - 1) * RB), :], s_mr.at[r])
        tot = jnp.sum(jnp.sum(nr[r], axis=0), axis=(0, 1), keepdims=True)
        denom = jnp.sqrt(tot) + NORM_EPS

        def init(k, _):
            rows = pl.ds(pl.multiple_of(k * RB, RB), RB)
            xo[r, rows, :] = (mr[r, rows, :].astype(F32) / denom).astype(BF16)
            return 0
        lax.fori_loop(0, G, init, 0)

        def step(_, carry):
            x = xo[r]
            a_s[...] = lax.dot_general(x, x, (((1,), (1,)), ((), ())), preferred_element_type=F32).astype(BF16)
            a = a_s[...]
            b_s[...] = (COEF_B * a.astype(F32) + COEF_C * jnp.dot(a, a, preferred_element_type=F32)).astype(BF16)
            xo[r] = (COEF_A * x.astype(F32) + jnp.dot(b_s[...], x, preferred_element_type=F32)).astype(BF16)
            return carry
        lax.fori_loop(0, NS_ITERS, step, 0)
        for j in range(1, G):
            dev = lax.rem(d + j, G)
            remote(xo.at[r, pl.ds(pl.multiple_of(dev * RB, RB), RB), :], orr.at[r, d], t_o.at[r], s_or.at[r], dev)
        orr[r, d] = xo[r, pl.ds(pl.multiple_of(d * RB, RB), RB), :]

    def wupd(r):
        s = r % 2
        drain(wi.at[s], l_w.at[r])
        drain(orr.at[r, pl.ds(0, G - 1)], s_or.at[r])
        if r >= 2:
            drain(wo.at[s], l_wo.at[r - 2])

        def body(k, _):
            w = wi[s, k]
            wo[s, k] = w - LEARN_RATE * (orr[r, k].astype(F32) * scale + WEIGHT_DECAY * w)
            return 0
        lax.fori_loop(0, NM, body, 0)
        pltpu.make_async_copy(wo.at[s], wn_ref.at[mats(r)], l_wo.at[r]).start()
        if r + 2 < R:
            load_w(r + 2)

    bar = pltpu.get_barrier_semaphore()
    for j in range(1, G):
        pl.semaphore_signal(bar, inc=1, device_id={'data': lax.rem(d + j, G)}, device_id_type=pl.DeviceIdType.MESH)
    pl.semaphore_wait(bar, G - 1)

    for r in range(min(2, R)):
        raw(r)
        load_relay(r)
        load_final(r)
        load_w(r)
    for r in range(R + 3):
        if r < R:
            relay(r)
        if r + 2 < R:
            raw(r + 2)
        if 0 <= r - 1 < R:
            final(r - 1)
        if 0 <= r - 2 < R:
            ns(r - 2)
        if 0 <= r - 3 < R:
            wupd(r - 3)
    for r in range(R):
        drain(g_ref.at[pl.ds(0, 6)], t_raw.at[r])
        drain(mb.at[r, pl.ds(0, G - 1)], t_m.at[r])
        drain(nso.at[r, pl.ds(0, G - 1)], t_n.at[r])
        drain(xo.at[r, pl.ds(0, (G - 1) * RB), :], t_o.at[r])
        if r >= R - 2:
            for q in range(2):
                drain(fo.at[r % 2, q], t_fo.at[r, q])
            drain(mo.at[r % 2], l_mo.at[r])
            drain(wo.at[r % 2], l_wo.at[r])


def solution(mesh):
    G = mesh.shape['data']
    row_spec = P('stage', 'data', None)
    grad_spec = P(('stage', 'data'), None, None, None)

    def local_step(w_rows, mom_rows, grad_full):
        n_mats, RB, C = w_rows.shape
        NM = G
        R = n_mats // NM
        H = RB // 2
        N = G * RB
        assert R * NM == n_mats and grad_full.shape[1:] == (n_mats, N, C) and N == C and G == 8
        dma = pltpu.SemaphoreType.DMA
        vm = pltpu.VMEM
        any_spec = pl.BlockSpec(memory_space=pl.ANY)
        out = jax.ShapeDtypeStruct(w_rows.shape, F32)
        w_new, mom_new = pl.pallas_call(
            functools.partial(muon_kernel, G, R),
            out_shape=(out, out),
            in_specs=[any_spec] * 3,
            out_specs=(any_spec, any_spec),
            scratch_shapes=[
                vm((R, 2, 3, NM, H, C), BF16),
                vm((2, 2, NM, H, C), BF16),
                vm((2, 2, NM, H, C), F32),
                vm((R, 2, NM, H, C), F32),
                vm((R, 2, 2, NM, H, C), BF16),
                vm((R, NM, RB, C), BF16),
                vm((2, NM, RB, C), BF16),
                vm((2, NM, RB, C), F32),
                vm((2, NM, RB, C), F32),
                vm((R, NM, RB, C), BF16),
                vm((R, N, C), BF16),
                vm((R, NM, 8, 128), F32),
                vm((R, NM, 8, 128), F32),
                vm((R, N, C), BF16),
                vm((R, NM, RB, C), BF16),
                vm((2, NM, RB, C), F32),
                vm((2, NM, RB, C), F32),
                vm((N, N), BF16),
                vm((N, N), BF16),
                dma((R, 2)), dma((R, 2)), dma((R,)), dma((R,)), dma((R,)), dma((R,)), dma((R,)),
                dma((R,)), dma((R, 2)), dma((R,)), dma((R,)), dma((R,)),
                dma((R,)), dma((R,)), dma((R,)), dma((R,)), dma((R,)), dma((R,)),
            ],
            compiler_params=pltpu.CompilerParams(collective_id=0, has_side_effects=True, vmem_limit_bytes=67043328),
            cost_estimate=pl.CostEstimate(flops=R * NS_ITERS * 6 * N * N * C, bytes_accessed=100 * 2 ** 20, transcendentals=0),
            name='muon',
        )(grad_full[0], w_rows, mom_rows)
        return w_new, mom_new

    return jax.shard_map(local_step, mesh=mesh, in_specs=(row_spec, row_spec, grad_spec), out_specs=(row_spec, row_spec), check_vma=False)
```

time: 490 us -> 295 us (0.60)
  Pallas kernels: 0 us -> 285 us
  waiting for transfers between devices: 250 us -> 0 us
  blocking collectives: 95.3 us -> 0 us
  matrix products: 74.2 us -> 0 us
  other arithmetic: 42.2 us -> 0 us
  between operations: 14.2 us -> 0.65 us
    pallas_call x0 -> x1, Pallas kernels: none -> 285 us  [local_step(): pl.pallas_call(functools.partial(muon_kernel, G, R), out_shape=(out, out)...]
    reduce_scatter x1 -> x0, waiting for transfers between devices: 250 us -> none  [local_step(): lax.psum_scatter(grad_full[0].astype(jnp.float32), 'data', scatter_dimens...]
    dot_general x10 -> x0, matrix products: 74.2 us -> none  [the longest x5 44.9 us: newton_schulz(): jnp.einsum('bij,bjk->bik', poly_mat, x_cur, preferred_element_type=jnp.fl...]
    all_to_all x1 -> x0, blocking collectives: 53.4 us -> none  [local_step(): x_rows = lax.all_to_all(x_ortho, 'data', 1, 0, tiled=True)]
    psum x1 -> x0, blocking collectives: 41.9 us -> none  [local_step(): lax.psum(jnp.sum(mom_new * mom_new, axis=(1, 2)), 'data')]
    convert_element_type x3 -> x0, other arithmetic: 30.2 us -> none  [the longest x1 27 us: local_step(): grad_full[0].astype(jnp.float32)]
    unnamed x12 -> x4, local copies, waits for them, and re-layouts: 2.73 us -> 9.6 us
    reduce_sum x1 -> x0, other arithmetic: 5.82 us -> none  [local_step(): jnp.sum(mom_new * mom_new, axis=(1, 2))]
  transfers between devices with their start and end apart: 2 -> 0, of which waited for: 1 -> 0; matrix products, arithmetic and copies ran while one was open for 0% -> 0% of each run, Pallas kernels for 0% -> 0%
where the time goes in v1:
time: 295 us
  Pallas kernels  285 us (97%)
  local copies, waits for them, and re-layouts  9.6 us (3%)
    pallas_call x1, Pallas kernels, local_step(): pl.pallas_call(functools.partial(muon_kernel, G, R), out_shape=(out, out)...  285 us
    unnamed x4, local copies, waits for them, and re-layouts  9.6 us

profile of v1, /device:TPU:81, one launch (start us, length us, event | category | flops | bytes accessed | tf_op | source)
XLA Modules:
  0.0 295.2 jit_solution(12906243932353129858)
XLA Ops:
  0.6 285.0 %muon.1 = (f32[48,64,512]{2,1,0:T(8,128)}, f32[48,64,512]{2,1,0:T(8,128)}) custom-call(bf16[48,512,512]{2,1,0:T(8,128)(2,1)} %bitcast.1, f32[48,64,512]{2,1,0:T(8,128)} %w_ref.1, f32[48,64,512]{2,1,0:T(8,128)} %m_ref.1), custom_call_target="tpu_custom_call" | custom-call | flops 24159191040 | bytes 104857600 | tf_op jit(solution)/shard_map/muon/pallas_call | solution.py:222
  285.6 0.0 copy-start
  285.6 6.9 %copy.7 = f32[48,64,512]{2,1,0:T(8,128)} copy(f32[48,64,512]{2,1,0:T(8,128)} %get-tuple-element.4) | data formatting | bytes 12582912
  292.5 0.0 copy-done
  292.5 2.7 copy.8
Async XLA Ops:
  285.6 6.9 %copy-start = (f32[48,64,512]{2,1,0:T(8,128)S(1)}, f32[48,64,512]{2,1,0:T(8,128)}, u32[]{:S(2)}) copy-start(f32[48,64,512]{2,1,0:T(8,128)} %get-tuple-element.5) | copy-start | bytes 18874372

commit v2 on v1

--- a/solution.py
+++ b/solution.py
@@ -20,10 +20,10 @@
 
 
 def muon_kernel(G, R, g_ref, w_ref, m_ref, wn_ref, mn_ref,
-                rl, orl, fo, fi, dr, po, ow, mi, mo, mb, mr, nso, nr, xo, orr, wi, wo, a_s, b_s,
+                rl, orl, fo, fi, dr, po, ow, mi, mb, mr, nso, nr, xo, orr, wi, a_s, b_s,
                 s_rl, s_fi, s_dr, s_po, s_mr, s_nr, s_or,
                 t_raw, t_fo, t_m, t_n, t_o,
-                l_rl, l_ow, l_m, l_w, l_mo, l_wo):
+                l_rl, l_ow, l_m, l_w):
     NM = G
     RB = mi.shape[2]
     H = RB // 2
@@ -100,8 +100,6 @@
         drain(dr.at[r], s_dr.at[r])
         for q in range(2):
             drain(fi.at[r, q], s_fi.at[r, q])
-        if r >= 2:
-            drain(mo.at[s], l_mo.at[r - 2])
 
         def body(k, _):
             part = jnp.zeros((8, 128), F32)
@@ -110,12 +108,12 @@
                 grad = ((dr[r, 1 - q, 0, k].astype(F32) + dr[r, 1 - q, 1, k].astype(F32))
                         + (po[r, k, rows, :].astype(F32) + ow[s, k, rows, :].astype(F32))) + fi[r, q, k]
                 new = MOMENTUM_COEF * mi[s, k, rows, :] + grad
-                mo[s, k, rows, :] = new
+                mn_ref[r * NM + k, rows, :] = new
                 mb[r, k, rows, :] = new.astype(BF16)
                 sq = jnp.sum((new * new).reshape(H // 8, 8, C), axis=0)
                 for j in range(C // 128):
                     part = part + sq[:, j * 128:(j + 1) * 128]
-            nso[r, k] = part
+            nso[r, k] = jnp.sum(part, axis=0, keepdims=True)
             return 0
         lax.fori_loop(0, NM, body, 0)
         mine = pl.ds(pl.multiple_of(d * RB, RB), RB)
@@ -125,7 +123,6 @@
             remote(mb.at[r, dev], mr.at[r, mine, :], t_m.at[r], s_mr.at[r], dev)
         mr[r, mine, :] = mb[r, d]
         nr[r, d] = nso[r, d]
-        pltpu.make_async_copy(mo.at[s], mn_ref.at[mats(r)], l_mo.at[r]).start()
         if r + 2 < R:
             load_final(r + 2)
 
@@ -149,6 +146,8 @@
             xo[r] = (COEF_A * x.astype(F32) + jnp.dot(b_s[...], x, preferred_element_type=F32)).astype(BF16)
             return carry
         lax.fori_loop(0, NS_ITERS, step, 0)
+
+    def osend(r):
         for j in range(1, G):
             dev = lax.rem(d + j, G)
             remote(xo.at[r, pl.ds(pl.multiple_of(dev * RB, RB), RB), :], orr.at[r, d], t_o.at[r], s_or.at[r], dev)
@@ -158,15 +157,12 @@
         s = r % 2
         drain(wi.at[s], l_w.at[r])
         drain(orr.at[r, pl.ds(0, G - 1)], s_or.at[r])
-        if r >= 2:
-            drain(wo.at[s], l_wo.at[r - 2])
 
         def body(k, _):
             w = wi[s, k]
-            wo[s, k] = w - LEARN_RATE * (orr[r, k].astype(F32) * scale + WEIGHT_DECAY * w)
+            wn_ref[r * NM + k] = w - LEARN_RATE * (orr[r, k].astype(F32) * scale + WEIGHT_DECAY * w)
             return 0
         lax.fori_loop(0, NM, body, 0)
-        pltpu.make_async_copy(wo.at[s], wn_ref.at[mats(r)], l_wo.at[r]).start()
         if r + 2 < R:
             load_w(r + 2)
 
@@ -180,17 +176,27 @@
         load_relay(r)
         load_final(r)
         load_w(r)
-    for r in range(R + 3):
-        if r < R:
-            relay(r)
+    for r in range(R):
+        relay(r)
         if r + 2 < R:
             raw(r + 2)
-        if 0 <= r - 1 < R:
+        if r >= 1:
             final(r - 1)
-        if 0 <= r - 2 < R:
+        if r >= 2:
             ns(r - 2)
-        if 0 <= r - 3 < R:
+            if r < R - 1:
+                osend(r - 2)
+        if r >= 3:
             wupd(r - 3)
+    final(R - 1)
+    osend(R - 3)
+    ns(R - 2)
+    osend(R - 2)
+    wupd(R - 3)
+    ns(R - 1)
+    osend(R - 1)
+    wupd(R - 2)
+    wupd(R - 1)
     for r in range(R):
         drain(g_ref.at[pl.ds(0, 6)], t_raw.at[r])
         drain(mb.at[r, pl.ds(0, G - 1)], t_m.at[r])
@@ -199,8 +205,18 @@
         if r >= R - 2:
             for q in range(2):
                 drain(fo.at[r % 2, q], t_fo.at[r, q])
-            drain(mo.at[r % 2], l_mo.at[r])
-            drain(wo.at[r % 2], l_wo.at[r])
+
+
+def store_kernel(parts, a_ref, b_ref, ao_ref, bo_ref, sem):
+    n = a_ref.shape[0] // parts
+    copies = []
+    for i in range(parts):
+        for j, (src, dst) in enumerate(((a_ref, ao_ref), (b_ref, bo_ref))):
+            copies.append(pltpu.make_async_copy(src.at[pl.ds(i * n, n)], dst.at[pl.ds(i * n, n)], sem.at[j, i]))
+    for cp in copies:
+        cp.start()
+    for cp in copies:
+        cp.wait()
 
 
 def solution(mesh):
@@ -218,12 +234,13 @@
         dma = pltpu.SemaphoreType.DMA
         vm = pltpu.VMEM
         any_spec = pl.BlockSpec(memory_space=pl.ANY)
-        out = jax.ShapeDtypeStruct(w_rows.shape, F32)
+        out = vm(w_rows.shape, F32)
+        vm_spec = pl.BlockSpec(memory_space=vm)
         w_new, mom_new = pl.pallas_call(
             functools.partial(muon_kernel, G, R),
             out_shape=(out, out),
             in_specs=[any_spec] * 3,
-            out_specs=(any_spec, any_spec),
+            out_specs=(vm_spec, vm_spec),
             scratch_shapes=[
                 vm((R, 2, 3, NM, H, C), BF16),
                 vm((2, 2, NM, H, C), BF16),
@@ -233,25 +250,33 @@
                 vm((R, NM, RB, C), BF16),
                 vm((2, NM, RB, C), BF16),
                 vm((2, NM, RB, C), F32),
-                vm((2, NM, RB, C), F32),
                 vm((R, NM, RB, C), BF16),
                 vm((R, N, C), BF16),
-                vm((R, NM, 8, 128), F32),
-                vm((R, NM, 8, 128), F32),
+                vm((R, NM, 1, 128), F32),
+                vm((R, NM, 1, 128), F32),
                 vm((R, N, C), BF16),
                 vm((R, NM, RB, C), BF16),
-                vm((2, NM, RB, C), F32),
                 vm((2, NM, RB, C), F32),
                 vm((N, N), BF16),
                 vm((N, N), BF16),
                 dma((R, 2)), dma((R, 2)), dma((R,)), dma((R,)), dma((R,)), dma((R,)), dma((R,)),
                 dma((R,)), dma((R, 2)), dma((R,)), dma((R,)), dma((R,)),
-                dma((R,)), dma((R,)), dma((R,)), dma((R,)), dma((R,)), dma((R,)),
+                dma((R,)), dma((R,)), dma((R,)), dma((R,)),
             ],
-            compiler_params=pltpu.CompilerParams(collective_id=0, has_side_effects=True, vmem_limit_bytes=67043328),
+            compiler_params=pltpu.CompilerParams(collective_id=0, has_side_effects=True, vmem_limit_bytes=50 * 2 ** 20),
             cost_estimate=pl.CostEstimate(flops=R * NS_ITERS * 6 * N * N * C, bytes_accessed=100 * 2 ** 20, transcendentals=0),
             name='muon',
         )(grad_full[0], w_rows, mom_rows)
-        return w_new, mom_new
+        parts = R
+        full = jax.ShapeDtypeStruct(w_rows.shape, F32)
+        return pl.pallas_call(
+            functools.partial(store_kernel, parts),
+            out_shape=(full, full),
+            in_specs=[vm_spec, vm_spec],
+            out_specs=(any_spec, any_spec),
+            scratch_shapes=[dma((2, parts))],
+            compiler_params=pltpu.CompilerParams(vmem_limit_bytes=2 ** 20),
+            name='store',
+        )(w_new, mom_new)
 
     return jax.shard_map(local_step, mesh=mesh, in_specs=(row_spec, row_spec, grad_spec), out_specs=(row_spec, row_spec), check_vma=False)

time: 295 us -> 288 us (0.976)
  local copies, waits for them, and re-layouts: 9.6 us -> 0 us
    unnamed x4 -> x0, local copies, waits for them, and re-layouts: 9.6 us -> none
    pallas_call x0 -> x1, Pallas kernels: none -> 4.67 us  [local_step(): pl.pallas_call(functools.partial(store_kernel, parts), out_shape=(full, f...]
where the time goes in v2:
time: 288 us
  Pallas kernels  287 us (100%)
    pallas_call x1, Pallas kernels, local_step(): pl.pallas_call(functools.partial(muon_kernel, G, R), out_shape=(out, out)...  283 us

profile of v2, /device:TPU:81, one launch (start us, length us, event | category | flops | bytes accessed | tf_op | source)
XLA Modules:
  0.0 288.1 jit_solution(17388812539087298518)
XLA Ops:
  0.6 282.8 %muon.1 = (f32[48,64,512]{2,1,0:T(8,128)S(1)}, f32[48,64,512]{2,1,0:T(8,128)S(1)}) custom-call(bf16[48,512,512]{2,1,0:T(8,128)(2,1)} %bitcast.1, f32[48,64,512]{2,1,0:T(8,128)} %w_ref.1, f32[48,64,512]{2,1,0:T(8,128)} %m_ref.1), custom_call_target="tpu_custom_call" | custom-call | flops 24159191040 | bytes 104857600 | tf_op jit(solution)/shard_map/muon/pallas_call | solution.py:239
  283.4 4.7 %store.1 = (f32[48,64,512]{2,1,0:T(8,128)}, f32[48,64,512]{2,1,0:T(8,128)}) custom-call(f32[48,64,512]{2,1,0:T(8,128)S(1)} %get-tuple-element.4.a_ref, f32[48,64,512]{2,1,0:T(8,128)S(1)} %get-tuple-element.5.b_ref), custom_call_target="tpu_custom_call" | custom-call | tf_op jit(solution)/shard_map/store/pallas_call | solution.py:272

commit v3 on v2

--- a/solution.py
+++ b/solution.py
@@ -15,6 +15,14 @@
 COEF_B = -4.7750
 COEF_C = 2.0315
 NS_ITERS = 5
+STORE_PARTS = 3
+ORDER = (
+    ('hop', 0), ('direct', 0), ('load', 0), ('load', 1), ('direct', 1), ('relay', 0), ('hop', 1), ('direct', 2), ('relay', 1),
+    ('direct', 3), ('hop', 2), ('direct', 4), ('hop', 3), ('hop', 4), ('final', 0), ('relay', 2), ('final', 1), ('relay', 3),
+    ('ns', 0), ('relay', 4), ('ns', 1), ('osend', 0), ('hop', 5), ('w', 0), ('osend', 1), ('final', 2), ('direct', 5),
+    ('final', 3), ('relay', 5), ('ns', 2), ('w', 1), ('final', 4), ('ns', 3), ('osend', 2), ('final', 5), ('osend', 3),
+    ('ns', 4), ('osend', 4), ('w', 2), ('ns', 5), ('osend', 5), ('w', 3), ('w', 4), ('w', 5),
+)
 F32 = jnp.float32
 BF16 = jnp.bfloat16
 
@@ -37,6 +45,7 @@
     left = lax.rem(p + chips - 1, chips)
     opp = lax.rem(p + 2, chips)
     partner = 2 * p + (1 - c)
+    others = (2 * opp, 2 * opp + 1, 2 * right, 2 * left, 2 * right + 1, 2 * left + 1, partner)
 
     def remote(src, dst, ssem, rsem, dev):
         pltpu.make_async_remote_copy(src_ref=src, dst_ref=dst, send_sem=ssem, recv_sem=rsem,
@@ -64,12 +73,19 @@
     def load_w(r):
         pltpu.make_async_copy(w_ref.at[mats(r)], wi.at[r % 2], l_w.at[r]).start()
 
-    def raw(r):
+    def load(r):
+        load_relay(r)
+        load_final(r)
+        load_w(r)
+
+    def raw_hop(r):
         for cc in range(2):
             remote(grows(r, 2 * opp + cc, 0), rl.at[r, 0, c], t_raw.at[r], s_rl.at[r, 0], 2 * right + cc)
             remote(grows(r, 2 * opp + cc, 1), rl.at[r, 1, c], t_raw.at[r], s_rl.at[r, 1], 2 * left + cc)
         remote(grows(r, 2 * right + (1 - c), 0), rl.at[r, 0, 2], t_raw.at[r], s_rl.at[r, 0], partner)
         remote(grows(r, 2 * left + (1 - c), 1), rl.at[r, 1, 2], t_raw.at[r], s_rl.at[r, 1], partner)
+
+    def raw_direct(r):
         for cc in range(2):
             remote(grows(r, 2 * right + cc, 1), dr.at[r, 0, c], t_raw.at[r], s_dr.at[r], 2 * right + cc)
             remote(grows(r, 2 * left + cc, 0), dr.at[r, 1, c], t_raw.at[r], s_dr.at[r], 2 * left + cc)
@@ -117,8 +133,7 @@
             return 0
         lax.fori_loop(0, NM, body, 0)
         mine = pl.ds(pl.multiple_of(d * RB, RB), RB)
-        for j in range(1, G):
-            dev = lax.rem(d + j, G)
+        for dev in others:
             remote(nso.at[r, dev], nr.at[r, d], t_n.at[r], s_nr.at[r], dev)
             remote(mb.at[r, dev], mr.at[r, mine, :], t_m.at[r], s_mr.at[r], dev)
         mr[r, mine, :] = mb[r, d]
@@ -148,8 +163,7 @@
         lax.fori_loop(0, NS_ITERS, step, 0)
 
     def osend(r):
-        for j in range(1, G):
-            dev = lax.rem(d + j, G)
+        for dev in others:
             remote(xo.at[r, pl.ds(pl.multiple_of(dev * RB, RB), RB), :], orr.at[r, d], t_o.at[r], s_or.at[r], dev)
         orr[r, d] = xo[r, pl.ds(pl.multiple_of(d * RB, RB), RB), :]
 
@@ -171,32 +185,9 @@
         pl.semaphore_signal(bar, inc=1, device_id={'data': lax.rem(d + j, G)}, device_id_type=pl.DeviceIdType.MESH)
     pl.semaphore_wait(bar, G - 1)
 
-    for r in range(min(2, R)):
-        raw(r)
-        load_relay(r)
-        load_final(r)
-        load_w(r)
-    for r in range(R):
-        relay(r)
-        if r + 2 < R:
-            raw(r + 2)
-        if r >= 1:
-            final(r - 1)
-        if r >= 2:
-            ns(r - 2)
-            if r < R - 1:
-                osend(r - 2)
-        if r >= 3:
-            wupd(r - 3)
-    final(R - 1)
-    osend(R - 3)
-    ns(R - 2)
-    osend(R - 2)
-    wupd(R - 3)
-    ns(R - 1)
-    osend(R - 1)
-    wupd(R - 2)
-    wupd(R - 1)
+    ops = dict(hop=raw_hop, direct=raw_direct, load=load, relay=relay, final=final, ns=ns, osend=osend, w=wupd)
+    for name, r in ORDER:
+        ops[name](r)
     for r in range(R):
         drain(g_ref.at[pl.ds(0, 6)], t_raw.at[r])
         drain(mb.at[r, pl.ds(0, G - 1)], t_m.at[r])
@@ -231,6 +222,7 @@
         H = RB // 2
         N = G * RB
         assert R * NM == n_mats and grad_full.shape[1:] == (n_mats, N, C) and N == C and G == 8
+        assert sorted(r for name, r in ORDER if name == 'w') == list(range(R))
         dma = pltpu.SemaphoreType.DMA
         vm = pltpu.VMEM
         any_spec = pl.BlockSpec(memory_space=pl.ANY)
@@ -267,14 +259,13 @@
             cost_estimate=pl.CostEstimate(flops=R * NS_ITERS * 6 * N * N * C, bytes_accessed=100 * 2 ** 20, transcendentals=0),
             name='muon',
         )(grad_full[0], w_rows, mom_rows)
-        parts = R
         full = jax.ShapeDtypeStruct(w_rows.shape, F32)
         return pl.pallas_call(
-            functools.partial(store_kernel, parts),
+            functools.partial(store_kernel, STORE_PARTS),
             out_shape=(full, full),
             in_specs=[vm_spec, vm_spec],
             out_specs=(any_spec, any_spec),
-            scratch_shapes=[dma((2, parts))],
+            scratch_shapes=[dma((2, STORE_PARTS))],
             compiler_params=pltpu.CompilerParams(vmem_limit_bytes=2 ** 20),
             name='store',
         )(w_new, mom_new)

time: 288 us -> 283 us (0.983)
  Pallas kernels: 287 us -> 282 us
    pallas_call x1, Pallas kernels: 283 us -> 278 us  [local_step(): pl.pallas_call(functools.partial(muon_kernel, G, R), out_shape=(out, out)...]
where the time goes in v3:
time: 283 us
  Pallas kernels  282 us (100%)
    pallas_call x1, Pallas kernels, local_step(): pl.pallas_call(functools.partial(muon_kernel, G, R), out_shape=(out, out)...  278 us

profile of v3, /device:TPU:81, one launch (start us, length us, event | category | flops | bytes accessed | tf_op | source)
XLA Modules:
  0.0 283.1 jit_solution(13482642700697256246)
XLA Ops:
  0.6 277.8 %muon.1 = (f32[48,64,512]{2,1,0:T(8,128)S(1)}, f32[48,64,512]{2,1,0:T(8,128)S(1)}) custom-call(bf16[48,512,512]{2,1,0:T(8,128)(2,1)} %bitcast.1, f32[48,64,512]{2,1,0:T(8,128)} %w_ref.1, f32[48,64,512]{2,1,0:T(8,128)} %m_ref.1), custom_call_target="tpu_custom_call" | custom-call | flops 24159191040 | bytes 104857600 | tf_op jit(solution)/shard_map/muon/pallas_call | solution.py:231
  278.4 4.6 %store.1 = (f32[48,64,512]{2,1,0:T(8,128)}, f32[48,64,512]{2,1,0:T(8,128)}) custom-call(f32[48,64,512]{2,1,0:T(8,128)S(1)} %get-tuple-element.4.a_ref, f32[48,64,512]{2,1,0:T(8,128)S(1)} %get-tuple-element.5.b_ref), custom_call_target="tpu_custom_call" | custom-call | tf_op jit(solution)/shard_map/store/pallas_call | solution.py:263

commit v4 on v3

--- a/solution.py
+++ b/solution.py
@@ -16,6 +16,7 @@
 COEF_C = 2.0315
 NS_ITERS = 5
 STORE_PARTS = 3
+NORM_SENDS = {1: 2, 3: 2, 4: 1, 5: 1}
 ORDER = (
     ('hop', 0), ('direct', 0), ('load', 0), ('load', 1), ('direct', 1), ('relay', 0), ('hop', 1), ('direct', 2), ('relay', 1),
     ('direct', 3), ('hop', 2), ('direct', 4), ('hop', 3), ('hop', 4), ('final', 0), ('relay', 2), ('final', 1), ('relay', 3),
@@ -27,11 +28,15 @@
 BF16 = jnp.bfloat16
 
 
-def muon_kernel(G, R, g_ref, w_ref, m_ref, wn_ref, mn_ref,
+def weight_step(w, x, scale):
+    return w - LEARN_RATE * (x.astype(F32) * scale + WEIGHT_DECAY * w)
+
+
+def muon_kernel(G, R, g_ref, w_ref, m_ref, wn_ref, mn_ref, wl_ref, xl_ref,
                 rl, orl, fo, fi, dr, po, ow, mi, mb, mr, nso, nr, xo, orr, wi, a_s, b_s,
                 s_rl, s_fi, s_dr, s_po, s_mr, s_nr, s_or,
                 t_raw, t_fo, t_m, t_n, t_o,
-                l_rl, l_ow, l_m, l_w):
+                l_rl, l_ow, l_m, l_w, stage, l_st):
     NM = G
     RB = mi.shape[2]
     H = RB // 2
@@ -71,7 +76,8 @@
         pltpu.make_async_copy(m_ref.at[mats(r)], mi.at[s], l_m.at[r]).start()
 
     def load_w(r):
-        pltpu.make_async_copy(w_ref.at[mats(r)], wi.at[r % 2], l_w.at[r]).start()
+        dst = wl_ref if r == R - 1 else wi.at[r % 2]
+        pltpu.make_async_copy(w_ref.at[mats(r)], dst, l_w.at[r]).start()
 
     def load(r):
         load_relay(r)
@@ -80,8 +86,9 @@
 
     def raw_hop(r):
         for cc in range(2):
-            remote(grows(r, 2 * opp + cc, 0), rl.at[r, 0, c], t_raw.at[r], s_rl.at[r, 0], 2 * right + cc)
-            remote(grows(r, 2 * opp + cc, 1), rl.at[r, 1, c], t_raw.at[r], s_rl.at[r, 1], 2 * left + cc)
+            for q, side in ((0, right), (1, left)):
+                rows = stage.at[q] if r == 0 and cc == 0 else grows(r, 2 * opp + cc, q)
+                remote(rows, rl.at[r, q, c], t_raw.at[r], s_rl.at[r, q], 2 * side + cc)
         remote(grows(r, 2 * right + (1 - c), 0), rl.at[r, 0, 2], t_raw.at[r], s_rl.at[r, 0], partner)
         remote(grows(r, 2 * left + (1 - c), 1), rl.at[r, 1, 2], t_raw.at[r], s_rl.at[r, 1], partner)
 
@@ -129,22 +136,26 @@
                 sq = jnp.sum((new * new).reshape(H // 8, 8, C), axis=0)
                 for j in range(C // 128):
                     part = part + sq[:, j * 128:(j + 1) * 128]
-            nso[r, k] = jnp.sum(part, axis=0, keepdims=True)
+            nso[k, r] = jnp.sum(part, axis=0, keepdims=True)
             return 0
         lax.fori_loop(0, NM, body, 0)
         mine = pl.ds(pl.multiple_of(d * RB, RB), RB)
         for dev in others:
-            remote(nso.at[r, dev], nr.at[r, d], t_n.at[r], s_nr.at[r], dev)
+            if r in NORM_SENDS:
+                batch = pl.ds(r + 1 - NORM_SENDS[r], NORM_SENDS[r])
+                remote(nso.at[dev, batch], nr.at[d, batch], t_n.at[r], s_nr.at[r], dev)
             remote(mb.at[r, dev], mr.at[r, mine, :], t_m.at[r], s_mr.at[r], dev)
         mr[r, mine, :] = mb[r, d]
-        nr[r, d] = nso[r, d]
+        nr[d, r] = nso[d, r]
         if r + 2 < R:
             load_final(r + 2)
 
     def ns(r):
-        drain(nr.at[r, pl.ds(0, G - 1)], s_nr.at[r])
+        for q in NORM_SENDS:
+            if q + 1 - NORM_SENDS[q] == r:
+                drain(nr.at[pl.ds(0, G - 1), pl.ds(0, NORM_SENDS[q])], s_nr.at[q])
         drain(mr.at[r, pl.ds(0, (G - 1) * RB), :], s_mr.at[r])
-        tot = jnp.sum(jnp.sum(nr[r], axis=0), axis=(0, 1), keepdims=True)
+        tot = jnp.sum(jnp.sum(nr[:, r], axis=0), axis=(0, 1), keepdims=True)
         denom = jnp.sqrt(tot) + NORM_EPS
 
         def init(k, _):
@@ -169,21 +180,27 @@
 
     def wupd(r):
         s = r % 2
-        drain(wi.at[s], l_w.at[r])
+        drain(wl_ref if r == R - 1 else wi.at[s], l_w.at[r])
         drain(orr.at[r, pl.ds(0, G - 1)], s_or.at[r])
 
         def body(k, _):
-            w = wi[s, k]
-            wn_ref[r * NM + k] = w - LEARN_RATE * (orr[r, k].astype(F32) * scale + WEIGHT_DECAY * w)
+            if r == R - 1:
+                xl_ref[k] = orr[r, k]
+            else:
+                wn_ref[r * NM + k] = weight_step(wi[s, k], orr[r, k], scale)
             return 0
         lax.fori_loop(0, NM, body, 0)
         if r + 2 < R:
             load_w(r + 2)
 
+    for q in range(2):
+        pltpu.make_async_copy(grows(0, 2 * opp, q), stage.at[q], l_st).start()
     bar = pltpu.get_barrier_semaphore()
-    for j in range(1, G):
-        pl.semaphore_signal(bar, inc=1, device_id={'data': lax.rem(d + j, G)}, device_id_type=pl.DeviceIdType.MESH)
-    pl.semaphore_wait(bar, G - 1)
+    peers = (2 * right, 2 * right + 1, 2 * left, 2 * left + 1, partner)
+    for dev in peers:
+        pl.semaphore_signal(bar, inc=1, device_id={'data': dev}, device_id_type=pl.DeviceIdType.MESH)
+    pl.semaphore_wait(bar, len(peers))
+    drain(stage, l_st)
 
     ops = dict(hop=raw_hop, direct=raw_direct, load=load, relay=relay, final=final, ns=ns, osend=osend, w=wupd)
     for name, r in ORDER:
@@ -191,22 +208,31 @@
     for r in range(R):
         drain(g_ref.at[pl.ds(0, 6)], t_raw.at[r])
         drain(mb.at[r, pl.ds(0, G - 1)], t_m.at[r])
-        drain(nso.at[r, pl.ds(0, G - 1)], t_n.at[r])
+        if r in NORM_SENDS:
+            drain(nso.at[pl.ds(0, G - 1), pl.ds(0, NORM_SENDS[r])], t_n.at[r])
         drain(xo.at[r, pl.ds(0, (G - 1) * RB), :], t_o.at[r])
         if r >= R - 2:
             for q in range(2):
                 drain(fo.at[r % 2, q], t_fo.at[r, q])
 
 
-def store_kernel(parts, a_ref, b_ref, ao_ref, bo_ref, sem):
-    n = a_ref.shape[0] // parts
+def store_kernel(scale, w_ref, m_ref, wl_ref, xl_ref, wo_ref, mo_ref, last, sem, last_sem):
     copies = []
-    for i in range(parts):
-        for j, (src, dst) in enumerate(((a_ref, ao_ref), (b_ref, bo_ref))):
-            copies.append(pltpu.make_async_copy(src.at[pl.ds(i * n, n)], dst.at[pl.ds(i * n, n)], sem.at[j, i]))
+    for j, (src, dst) in enumerate(((m_ref, mo_ref), (w_ref, wo_ref))):
+        n = src.shape[0]
+        for i in range(STORE_PARTS):
+            rows = pl.ds(n * i // STORE_PARTS, n * (i + 1) // STORE_PARTS - n * i // STORE_PARTS)
+            copies.append(pltpu.make_async_copy(src.at[rows], dst.at[rows], sem.at[j, i]))
     for cp in copies:
         cp.start()
-    for cp in copies:
+
+    def body(k, _):
+        last[k] = weight_step(wl_ref[k], xl_ref[k], scale)
+        return 0
+    lax.fori_loop(0, last.shape[0], body, 0)
+    cp = pltpu.make_async_copy(last, wo_ref.at[pl.ds(w_ref.shape[0], last.shape[0])], last_sem)
+    cp.start()
+    for cp in copies + [cp]:
         cp.wait()
 
 
@@ -226,13 +252,13 @@
         dma = pltpu.SemaphoreType.DMA
         vm = pltpu.VMEM
         any_spec = pl.BlockSpec(memory_space=pl.ANY)
-        out = vm(w_rows.shape, F32)
+        out = (vm(((R - 1) * NM, RB, C), F32), vm(w_rows.shape, F32), vm((NM, RB, C), F32), vm((NM, RB, C), BF16))
         vm_spec = pl.BlockSpec(memory_space=vm)
-        w_new, mom_new = pl.pallas_call(
+        results = pl.pallas_call(
             functools.partial(muon_kernel, G, R),
-            out_shape=(out, out),
+            out_shape=out,
             in_specs=[any_spec] * 3,
-            out_specs=(vm_spec, vm_spec),
+            out_specs=(vm_spec,) * 4,
             scratch_shapes=[
                 vm((R, 2, 3, NM, H, C), BF16),
                 vm((2, 2, NM, H, C), BF16),
@@ -244,8 +270,8 @@
                 vm((2, NM, RB, C), F32),
                 vm((R, NM, RB, C), BF16),
                 vm((R, N, C), BF16),
-                vm((R, NM, 1, 128), F32),
-                vm((R, NM, 1, 128), F32),
+                vm((G, R, 1, 128), F32),
+                vm((G, R, 1, 128), F32),
                 vm((R, N, C), BF16),
                 vm((R, NM, RB, C), BF16),
                 vm((2, NM, RB, C), F32),
@@ -254,6 +280,7 @@
                 dma((R, 2)), dma((R, 2)), dma((R,)), dma((R,)), dma((R,)), dma((R,)), dma((R,)),
                 dma((R,)), dma((R, 2)), dma((R,)), dma((R,)), dma((R,)),
                 dma((R,)), dma((R,)), dma((R,)), dma((R,)),
+                vm((2, NM, H, C), BF16), dma(()),
             ],
             compiler_params=pltpu.CompilerParams(collective_id=0, has_side_effects=True, vmem_limit_bytes=50 * 2 ** 20),
             cost_estimate=pl.CostEstimate(flops=R * NS_ITERS * 6 * N * N * C, bytes_accessed=100 * 2 ** 20, transcendentals=0),
@@ -261,13 +288,13 @@
         )(grad_full[0], w_rows, mom_rows)
         full = jax.ShapeDtypeStruct(w_rows.shape, F32)
         return pl.pallas_call(
-            functools.partial(store_kernel, STORE_PARTS),
+            functools.partial(store_kernel, 0.2 * math.sqrt(max(N, C))),
             out_shape=(full, full),
-            in_specs=[vm_spec, vm_spec],
+            in_specs=[vm_spec] * 4,
             out_specs=(any_spec, any_spec),
-            scratch_shapes=[dma((2, STORE_PARTS))],
-            compiler_params=pltpu.CompilerParams(vmem_limit_bytes=2 ** 20),
+            scratch_shapes=[vm((NM, RB, C), F32), dma((2, STORE_PARTS)), dma(())],
+            compiler_params=pltpu.CompilerParams(vmem_limit_bytes=2 ** 21),
             name='store',
-        )(w_new, mom_new)
+        )(*results)
 
     return jax.shard_map(local_step, mesh=mesh, in_specs=(row_spec, row_spec, grad_spec), out_specs=(row_spec, row_spec), check_vma=False)

time: 283 us -> 282 us (level)
  no operation moved by 1% of the time
where the time goes in v4:
time: 282 us
  Pallas kernels  282 us (100%)
    pallas_call x1, Pallas kernels, local_step(): pl.pallas_call(functools.partial(muon_kernel, G, R), out_shape=out, in_sp...  277 us

profile of v4, /device:TPU:81, one launch (start us, length us, event | category | flops | bytes accessed | tf_op | source)
XLA Modules:
  0.0 282.2 jit_solution(2194930874889917510)
XLA Ops:
  0.6 277.0 %muon.1 = (f32[40,64,512]{2,1,0:T(8,128)S(1)}, f32[48,64,512]{2,1,0:T(8,128)S(1)}, f32[8,64,512]{2,1,0:T(8,128)S(1)}, bf16[8,64,512]{2,1,0:T(8,128)(2,1)S(1)}) custom-call(bf16[48,512,512]{2,1,0:T(8,128)(2,1)} %bitcast.1, f32[48,64,512]{2,1,0:T(8,128)} %w_ref.1, f32[48,64,512]{2,1,0:T(8,128)} %m_ref.1), custom_call_target="tpu_custom_call" | custom-call | flops 24159191040 | bytes 104857600 | tf_op jit(solution)/shard_map/muon/pallas_call | solution.py:257
  277.6 4.6 %store.1 = (f32[48,64,512]{2,1,0:T(8,128)}, f32[48,64,512]{2,1,0:T(8,128)}) custom-call(f32[40,64,512]{2,1,0:T(8,128)S(1)} %get-tuple-element.6.w_ref, f32[48,64,512]{2,1,0:T(8,128)S(1)} %get-tuple-element.7.m_ref, f32[8,64,512]{2,1,0:T(8,128)S(1)} %get-tuple-element.8.wl_ref, bf16[8,64,512]{2,1,0:T(8,128)(2,1)S(1)} %get-tuple-element.9.xl_ref), custom_call_target="tpu_custom_call" | custom-call | tf_op jit(solution)/shard_map/store/pallas_call | solution.py:290

commit v5 on v4

--- a/solution.py
+++ b/solution.py
@@ -36,7 +36,7 @@
                 rl, orl, fo, fi, dr, po, ow, mi, mb, mr, nso, nr, xo, orr, wi, a_s, b_s,
                 s_rl, s_fi, s_dr, s_po, s_mr, s_nr, s_or,
                 t_raw, t_fo, t_m, t_n, t_o,
-                l_rl, l_ow, l_m, l_w, stage, l_st):
+                l_rl, l_ow, l_m, l_w):
     NM = G
     RB = mi.shape[2]
     H = RB // 2
@@ -50,7 +50,7 @@
     left = lax.rem(p + chips - 1, chips)
     opp = lax.rem(p + 2, chips)
     partner = 2 * p + (1 - c)
-    others = (2 * opp, 2 * opp + 1, 2 * right, 2 * left, 2 * right + 1, 2 * left + 1, partner)
+    others = (2 * opp + 1, 2 * right + 1, 2 * left + 1, 2 * opp, 2 * right, 2 * left, partner)
 
     def remote(src, dst, ssem, rsem, dev):
         pltpu.make_async_remote_copy(src_ref=src, dst_ref=dst, send_sem=ssem, recv_sem=rsem,
@@ -87,7 +87,7 @@
     def raw_hop(r):
         for cc in range(2):
             for q, side in ((0, right), (1, left)):
-                rows = stage.at[q] if r == 0 and cc == 0 else grows(r, 2 * opp + cc, q)
+                rows = grows(r, 2 * opp + cc, q)
                 remote(rows, rl.at[r, q, c], t_raw.at[r], s_rl.at[r, q], 2 * side + cc)
         remote(grows(r, 2 * right + (1 - c), 0), rl.at[r, 0, 2], t_raw.at[r], s_rl.at[r, 0], partner)
         remote(grows(r, 2 * left + (1 - c), 1), rl.at[r, 1, 2], t_raw.at[r], s_rl.at[r, 1], partner)
@@ -175,32 +175,32 @@
 
     def osend(r):
         for dev in others:
-            remote(xo.at[r, pl.ds(pl.multiple_of(dev * RB, RB), RB), :], orr.at[r, d], t_o.at[r], s_or.at[r], dev)
-        orr[r, d] = xo[r, pl.ds(pl.multiple_of(d * RB, RB), RB), :]
+            remote(xo.at[r, pl.ds(pl.multiple_of(dev * RB, RB), RB), :], (xl_ref if r == R - 1 else orr.at[r]).at[d], t_o.at[r], s_or.at[r], dev)
+        own = xo[r, pl.ds(pl.multiple_of(d * RB, RB), RB), :]
+        if r == R - 1:
+            xl_ref[d] = own
+        else:
+            orr[r, d] = own
 
     def wupd(r):
         s = r % 2
         drain(wl_ref if r == R - 1 else wi.at[s], l_w.at[r])
-        drain(orr.at[r, pl.ds(0, G - 1)], s_or.at[r])
+        drain((xl_ref if r == R - 1 else orr.at[r]).at[pl.ds(0, G - 1)], s_or.at[r])
+        if r == R - 1:
+            return
 
         def body(k, _):
-            if r == R - 1:
-                xl_ref[k] = orr[r, k]
-            else:
-                wn_ref[r * NM + k] = weight_step(wi[s, k], orr[r, k], scale)
+            wn_ref[r * NM + k] = weight_step(wi[s, k], orr[r, k], scale)
             return 0
         lax.fori_loop(0, NM, body, 0)
         if r + 2 < R:
             load_w(r + 2)
 
-    for q in range(2):
-        pltpu.make_async_copy(grows(0, 2 * opp, q), stage.at[q], l_st).start()
     bar = pltpu.get_barrier_semaphore()
     peers = (2 * right, 2 * right + 1, 2 * left, 2 * left + 1, partner)
     for dev in peers:
         pl.semaphore_signal(bar, inc=1, device_id={'data': dev}, device_id_type=pl.DeviceIdType.MESH)
     pl.semaphore_wait(bar, len(peers))
-    drain(stage, l_st)
 
     ops = dict(hop=raw_hop, direct=raw_direct, load=load, relay=relay, final=final, ns=ns, osend=osend, w=wupd)
     for name, r in ORDER:
@@ -280,7 +280,6 @@
                 dma((R, 2)), dma((R, 2)), dma((R,)), dma((R,)), dma((R,)), dma((R,)), dma((R,)),
                 dma((R,)), dma((R, 2)), dma((R,)), dma((R,)), dma((R,)),
                 dma((R,)), dma((R,)), dma((R,)), dma((R,)),
-                vm((2, NM, H, C), BF16), dma(()),
             ],
             compiler_params=pltpu.CompilerParams(collective_id=0, has_side_effects=True, vmem_limit_bytes=50 * 2 ** 20),
             cost_estimate=pl.CostEstimate(flops=R * NS_ITERS * 6 * N * N * C, bytes_accessed=100 * 2 ** 20, transcendentals=0),

time: 282 us -> 281 us (level)
  no operation moved by 1% of the time
where the time goes in v5:
time: 281 us
  Pallas kernels  280 us (100%)
    pallas_call x1, Pallas kernels, local_step(): pl.pallas_call(functools.partial(muon_kernel, G, R), out_shape=out, in_sp...  275 us

profile of v5, /device:TPU:81, one launch (start us, length us, event | category | flops | bytes accessed | tf_op | source)
XLA Modules:
  0.0 280.6 jit_solution(7195873419156844799)
XLA Ops:
  0.6 275.3 %muon.1 = (f32[40,64,512]{2,1,0:T(8,128)S(1)}, f32[48,64,512]{2,1,0:T(8,128)S(1)}, f32[8,64,512]{2,1,0:T(8,128)S(1)}, bf16[8,64,512]{2,1,0:T(8,128)(2,1)S(1)}) custom-call(bf16[48,512,512]{2,1,0:T(8,128)(2,1)} %bitcast.1, f32[48,64,512]{2,1,0:T(8,128)} %w_ref.1, f32[48,64,512]{2,1,0:T(8,128)} %m_ref.1), custom_call_target="tpu_custom_call" | custom-call | flops 24159191040 | bytes 104857600 | tf_op jit(solution)/shard_map/muon/pallas_call | solution.py:257
  275.9 4.6 %store.1 = (f32[48,64,512]{2,1,0:T(8,128)}, f32[48,64,512]{2,1,0:T(8,128)}) custom-call(f32[40,64,512]{2,1,0:T(8,128)S(1)} %get-tuple-element.6.w_ref, f32[48,64,512]{2,1,0:T(8,128)S(1)} %get-tuple-element.7.m_ref, f32[8,64,512]{2,1,0:T(8,128)S(1)} %get-tuple-element.8.wl_ref, bf16[8,64,512]{2,1,0:T(8,128)(2,1)S(1)} %get-tuple-element.9.xl_ref), custom_call_target="tpu_custom_call" | custom-call | tf_op jit(solution)/shard_map/store/pallas_call | solution.py:289
